TPU v7x, 32 devices: a whole 2x2x4 slice. The times are simulated.
32 devices in a mesh: section: 8 (over z, x), tensor: 4 (over y, core).
Axes of the slice: x: 2, y: 2, z: 4, core: 2. Of those that a mesh axis runs over, the one named last changes fastest.
Arguments:
- hidden: bfloat16 [32, 8192], P(('section', 'tensor')), may hold values from -12 to 12
- weight: bfloat16 [16384, 8192], P(('section', 'tensor')), may hold values from -1 to 1
- targets: int32 [32], replicated, may hold values from 0 to 16383
- loss_grad: float32 [32], P(('section', 'tensor')), may hold values from 8 to 64
Outputs:
- token_loss: float32 [32], P(('section', 'tensor'))
- hidden_grad: bfloat16 [32, 8192], P(('section', 'tensor'))
All inputs are finite; a program needn't handle non-finite values.
Results may differ from a plain program's by a relative error of at most 0.0039.
Values may be sent and summed in bfloat16 or wider, within the bound.
A program may use at most 64 MiB of HBM per device.

v0:
```python
import jax
import jax.numpy as jnp
from jax import lax
from jax.sharding import PartitionSpec as P


def joined(array, axis, combine):
    everything = jax.tree.map(lambda part: lax.all_gather(part, axis), array)
    initial = jax.tree.map(lambda part: part[0], everything)

    def lap(k, so_far):
        return combine(so_far, jax.tree.map(lambda part: part[k], everything))

    return lax.fori_loop(1, lax.axis_size(axis), lap, initial)


def combine_parts(left_part, right_part):
    largest = jnp.maximum(left_part[0], right_part[0])
    summed = left_part[1] * jnp.exp(left_part[0] - largest) + right_part[1] * jnp.exp(
        right_part[0] - largest
    )
    return (largest, summed, left_part[2] + right_part[2])


def shards(hidden, weight, targets, loss_grad):
    tok_dev = hidden.shape[0]
    vocab_dev = weight.shape[0]
    logits = lax.dot_general(
        lax.all_gather(hidden, ("section", "tensor"), axis=0, tiled=True),
        weight,
        (((1,), (1,)), ((), ())),
        preferred_element_type=jnp.float32,
    )
    my_index = lax.axis_index(("section", "tensor"))
    offset = my_index * vocab_dev
    columns = offset + lax.broadcasted_iota(jnp.int32, (1, vocab_dev), 1)
    target_mask = columns == targets[:, None]
    local_target = jnp.sum(jnp.where(target_mask, logits, 0.0), axis=1)
    local_max = jnp.max(logits, axis=1)
    local_shift = jnp.exp(logits - local_max[:, None])
    local_total = jnp.sum(local_shift, axis=1)
    row_max, exp_total, target_logit = joined(
        (local_max, local_total, local_target), ("section", "tensor"), combine_parts
    )
    shifted = local_shift * jnp.exp(local_max - row_max)[:, None]
    probs_grad = (shifted / exp_total[:, None] - target_mask.astype(jnp.float32)).astype(
        jnp.bfloat16
    )
    all_loss = row_max + jnp.log(exp_total) - target_logit
    token_loss = lax.dynamic_slice_in_dim(all_loss, my_index * tok_dev, tok_dev)
    grad_sum = lax.psum_scatter(
        jnp.dot(probs_grad, weight, preferred_element_type=jnp.float32),
        ("section", "tensor"),
        scatter_dimension=0,
        tiled=True,
    )
    hidden_grad = (loss_grad[:, None] * grad_sum).astype(jnp.bfloat16)
    return (token_loss, hidden_grad)


def solution(mesh):
    return jax.shard_map(
        shards,
        mesh=mesh,
        in_specs=(
            P(("section", "tensor"), None),
            P(("section", "tensor"), None),
            P(),
            P(("section", "tensor")),
        ),
        out_specs=(P(("section", "tensor")), P(("section", "tensor"), None)),
        check_vma=False,
    )
```

profile of v0, /device:TPU:0, one launch (start us, length us, event | category | flops | bytes accessed | tf_op | source)
XLA Modules:
  0.0 245.1 jit_solution(3485604667387452103)
XLA Ops:
  7.2 0.0 copy-start
  7.2 0.0 all-reduce.7.cloned.1.call-start
  7.2 46.4 %all-gather.3 = bf16[32,1,8192]{2,1,0:T(2,128)(2,1)S(1)} all-gather(bf16[1,1,8192]{2,1,0:T(2,128)(2,1)} %bitcast.29), channel_id=1, replica_groups=mesh['section'=8,'tensor'=4] {'section','tensor'}, dimensions={0}, use_global_device_ids=true | all-gather | bytes 540672 | tf_op jit(solution)/shard_map/all_gather | solution.py:29
  53.6 6.1 %fusion.23 = (f32[32]{0:T(128)S(1)}, f32[32,512]{1,0:T(8,128)S(1)}) fusion(bf16[512,8192]{1,0:T(8,128)(2,1)} %param.7, bf16[32,1,8192]{2,1,0:T(2,128)(2,1)S(1)} %all-gather.3), kind=kOutput, calls=%fused_computation.31 | convolution fusion | flops 268451808 | bytes 8978560 | tf_op jit(solution)/shard_map/dot_general | solution.py:28
  59.7 0.2 dynamic-update-slice
  60.0 0.0 copy-done
  60.0 0.2 fusion.10
  60.2 0.2 dynamic-update-slice.1
  60.4 0.2 dynamic-update-slice.2
  60.6 37.0 %all-reduce.4 = (f32[1024]{0:T(1024)S(1)}, f32[1024]{0:T(1024)S(1)}, f32[1024]{0:T(1024)S(1)}) all-reduce(f32[1024]{0:T(1024)S(1)} %dynamic-update-slice, f32[1024]{0:T(1024)S(1)} %dynamic-update-slice.1, f32[1024]{0:T(1024)S(1)} %dynamic-update-slice.2), channel_id=2, replica_groups=mesh['section'=8,'tensor'=4] {'section','tensor'}, use_global_device_ids=true, to_apply=%add | all-reduce | flops 3072 | bytes 24576
  97.6 0.1 reshape.16
  97.7 0.1 reshape.17
  97.8 0.1 reshape.18
  97.8 1.4 while.19
  99.3 6.0 %fusion.14 = f32[32,8192]{1,0:T(8,128)} fusion(bf16[512,8192]{1,0:T(8,128)(2,1)} %param.7, f32[32,512]{1,0:T(8,128)S(1)} %get-tuple-element.208, f32[32]{0:T(128)S(1)} %get-tuple-element.181, f32[32]{0:T(128)S(1)} %get-tuple-element.205, s32[512]{0:T(512)S(1)} %iota_add_fusion, f32[32]{0:T(128)S(1)} %get-tuple-element.207, s32[32]{0:T(128)S(1)} %copy-done), kind=kOutput, calls=%fused_computation.20 | convolution fusion | flops 268550144 | bytes 9505280 | tf_op jit(solution)/shard_map/dot_general | solution.py:52
  105.3 0.0 all-reduce.7.cloned.1.call-update
  106.0 0.6 dynamic_slice.33
  106.6 130.1 %all-reduce.7.cloned.1.call-done = f32[32,8192]{1,0:T(8,128)} async-done(((f32[32,8192]{1,0:T(8,128)}), f32[32,8192]{1,0:T(8,128)}) %all-reduce.7.cloned.1.call-update) | async-done | bytes 1048592
  236.7 1.6 fusion.16
  (39 shorter events, 0.9 us)
Async XLA Ops:
  7.2 52.8 %copy-start = (s32[32]{0:T(128)S(1)}, s32[32]{0:T(128)}, u32[]{:S(2)}) copy-start(s32[32]{0:T(128)} %param.8) | copy-start | bytes 388
  7.2 229.5 %all-reduce.7.cloned.1.call-start = ((), (), s32[]{:S(2)}) async-start(), calls=%async_computation | async-start | bytes 2097152
Sparse Core Ops, SparseCore 0:
  105.5 131.1 all-reduce.6
where the time goes:
time: 245 us
  waiting for transfers between devices  130 us (53%)
  blocking collectives  83.4 us (34%)
  between operations  14.7 us (6%)
  matrix products  12.1 us (5%)
  other arithmetic  2.69 us (1%)
    unnamed x2, waiting for transfers between devices  130 us
    all_gather x1, blocking collectives, shards(): lax.all_gather(hidden, ('section', 'tensor'), axis=0, tiled=True)  46.4 us
    unnamed x1, blocking collectives  37 us
    dot_general x1, matrix products, shards(): lax.dot_general(lax.all_gather(hidden, ('section', 'tensor'), axis=0, til...  6.1 us
    dot_general x1, matrix products, shards(): jnp.dot(probs_grad, weight, preferred_element_type=jnp.float32)  6.03 us
  transfers between devices with their start and end apart: 1, of which 1 were waited for; matrix products, arithmetic and copies ran while one was open for 0% of the time, Pallas kernels for 0%

commit v1 on v0

v1 whole, which is shorter than its diff:
```python
import functools

import jax
import jax.numpy as jnp
from jax import lax
from jax.experimental import pallas as pl
from jax.experimental.pallas import tpu as pltpu
from jax.sharding import PartitionSpec as P

MESH = pl.DeviceIdType.MESH
LANES = 128
GROUP = 8


def kernel(S, T, hid_ref, w_hbm, tgt_ref, lg_ref, loss_ref, out_ref,
           wv, hbuf, slab, gt, sendbuf, rbuf, rowbuf, st_send, st_recv,
           w_sem, ag_send, ag_recv, st_ssem, st_rsem, rs_send, rs_recv):
    n = S * T
    H = T // 2
    V, D = wv.shape
    C = D // LANES
    L = st_send.shape[2]
    s = lax.axis_index("section")
    t = lax.axis_index("tensor")
    me = s * T + t
    pt = t + 1 - 2 * lax.rem(t, 2)

    def sec(k):
        return lax.rem(s + k + S, S)

    def ten(j):
        return lax.rem(t + 2 * j + T, T)

    parts = w_sem.shape[0]
    rows = V // parts

    def w_copy(q):
        r = pl.ds(q * rows, rows)
        return pltpu.make_async_copy(w_hbm.at[r], wv.at[r], w_sem.at[q])

    for q in range(parts):
        w_copy(q).start()

    barrier = pltpu.get_barrier_semaphore()

    def greet(k, _):
        o = lax.rem(me + k, n)
        pl.semaphore_signal(barrier, inc=1, device_id=(o // T, lax.rem(o, T)), device_id_type=MESH)
        return 0

    lax.fori_loop(1, n, greet, 0)

    own = hid_ref[...].astype(jnp.float32)
    for c in range(C):
        rowbuf[c:c + 1, :] = own[:, c * LANES:(c + 1) * LANES]
    hbuf[me] = rowbuf[...].astype(jnp.bfloat16)

    pl.semaphore_wait(barrier, n - 1)

    def ag(tok, ds, dt):
        pltpu.make_async_remote_copy(
            src_ref=hbuf.at[tok], dst_ref=hbuf.at[tok], send_sem=ag_send,
            recv_sem=ag_recv.at[tok], device_id=(ds, dt), device_id_type=MESH).start()

    def landed(buf, sem, i):
        pltpu.make_async_copy(buf.at[i], buf.at[i], sem.at[i]).wait()

    def forward(tok):
        for j in range(1, H):
            ag(tok, s, ten(j))
        ag(tok, s, pt)

    def p1(k, _):
        ag(me, sec(k), t)
        return 0

    lax.fori_loop(1, S, p1, 0)
    forward(me)

    def p2(k, _):
        tok = sec(-k) * T + t
        landed(hbuf, ag_recv, tok)
        forward(tok)
        return 0

    lax.fori_loop(1, S, p2, 0)
    for j in range(1, H):
        def p3(k, _, j=j):
            tok = sec(-k) * T + ten(-j)
            landed(hbuf, ag_recv, tok)
            ag(tok, s, pt)
            return 0

        lax.fori_loop(0, S, p3, 0)

    tcol = lax.fori_loop(
        0, n, lambda i, x: jnp.where(lax.broadcasted_iota(jnp.int32, (n, LANES), 0) == i, tgt_ref[i], x),
        jnp.zeros((n, LANES), jnp.int32))[:, :1]

    for j in range(H):
        def p4(k, _, j=j):
            tok = sec(-k) * T + lax.rem(pt + 2 * j, T)
            landed(hbuf, ag_recv, tok)
            return 0

        lax.fori_loop(0, S, p4, 0)

    def widen(i, _):
        slab[pl.ds(pl.multiple_of(i * C, C), C), :] = hbuf[i].astype(jnp.float32)
        return 0

    lax.fori_loop(0, n, widen, 0)
    for q in range(parts):
        w_copy(q).wait()

    KC = GROUP * LANES

    def dot1(kc, acc):
        lhs = jnp.concatenate(
            [slab[pl.ds(kc * GROUP + i, n, stride=C), :] for i in range(GROUP)], axis=1).astype(jnp.bfloat16)
        w = wv[:, pl.ds(pl.multiple_of(kc * KC, KC), KC)]
        return acc + lax.dot_general(lhs, w, (((1,), (1,)), ((), ())), preferred_element_type=jnp.float32)

    logits = lax.fori_loop(0, D // KC, dot1, jnp.zeros((n, V), jnp.float32))

    mask = lax.broadcasted_iota(jnp.int32, (n, V), 1) + me * V == tcol
    m = jnp.max(logits, axis=1, keepdims=True)
    e = jnp.exp(logits - m)
    total = jnp.sum(e, axis=1, keepdims=True)
    tl = jnp.sum(jnp.where(mask, logits, 0.0), axis=1, keepdims=True)
    ptl = jnp.sum(jnp.where(mask, e, 0.0), axis=1, keepdims=True)

    r = lax.broadcasted_iota(jnp.int32, (n, L), 0)
    c = lax.broadcasted_iota(jnp.int32, (n, L), 1)
    packed = jnp.where(c == r, m, jnp.where(c == r + n, total, jnp.where(c == r + 2 * n, tl, 0.0)))
    packed = jnp.sum(packed, axis=0, keepdims=True)
    st_send[0] = packed
    st_recv[0] = packed

    def share(k, _):
        o = lax.rem(me + k, n)
        pltpu.make_async_remote_copy(
            src_ref=st_send.at[0], dst_ref=st_recv.at[k], send_sem=st_ssem, recv_sem=st_rsem,
            device_id=(o // T, lax.rem(o, T)), device_id_type=MESH).start()
        return 0

    lax.fori_loop(1, n, share, 0)

    lhs2 = jnp.concatenate(
        [jnp.where(mask, 0.0, e), mask.astype(jnp.float32)], axis=0).astype(jnp.bfloat16)

    def dot2(kc, _):
        cols = pl.ds(pl.multiple_of(kc * KC, KC), KC)
        gt[:, cols] = jnp.dot(lhs2, wv[:, cols], preferred_element_type=jnp.float32)
        return 0

    lax.fori_loop(0, D // KC, dot2, 0)

    others = st_recv.at[pl.ds(1, n - 1)]
    pltpu.make_async_copy(others, others, st_rsem).wait()

    top = lax.fori_loop(1, n, lambda k, x: jnp.maximum(x, st_recv[k]), st_recv[0])

    lane = lax.broadcasted_iota(jnp.int32, (1, L), 1)
    live = lane < n
    top = jnp.where(live, top, 0.0)

    def add_live(k, carry):
        z, g = carry
        row = st_recv[k]
        gap = jnp.where(live, row - top, 0.0)
        return z + jnp.exp(gap) * pltpu.roll(row, L - n, 1), g + pltpu.roll(row, L - 2 * n, 1)

    z, g = lax.fori_loop(0, n, add_live, (jnp.zeros((1, L), jnp.float32), jnp.zeros((1, L), jnp.float32)))
    z = jnp.where(live, z, 1.0)
    loss_ref[0] = jnp.sum(jnp.where(lane == me, top + jnp.log(z) - g, 0.0))
    top_c = jnp.sum(jnp.where(c == r, top, 0.0), axis=1, keepdims=True)
    z_c = jnp.sum(jnp.where(c == r, z, 0.0), axis=1, keepdims=True)
    scale = jnp.exp(m - top_c) / z_c
    hit = ptl * scale - 1.0

    def spread(kc, _):
        for i in range(GROUP):
            cols = pl.ds(pl.multiple_of(kc * KC + i * LANES, LANES), LANES)
            slab[pl.ds(kc * GROUP + i, n, stride=C), :] = scale * gt[:n, cols] + hit * gt[n:, cols]
        return 0

    lax.fori_loop(0, D // KC, spread, 0)

    def part(tok):
        return slab[pl.ds(pl.multiple_of(tok * C, C), C), :]

    def rs(tok, slot, value, ds, dt):
        sendbuf[tok] = value.astype(jnp.bfloat16)
        pltpu.make_async_remote_copy(
            src_ref=sendbuf.at[tok], dst_ref=rbuf.at[slot], send_sem=rs_send,
            recv_sem=rs_recv.at[slot], device_id=(ds, dt), device_id_type=MESH).start()

    def got(slot):
        landed(rbuf, rs_recv, slot)
        return rbuf[slot].astype(jnp.float32)

    for j in [*range(1, H), 0]:
        def qa(k, _, j=j):
            tok = sec(k + 1) * T + lax.rem(pt + 2 * j, T)
            rs(tok, tok, part(tok), s, pt)
            return 0

        lax.fori_loop(0, S, qa, 0)

    for j in range(1, H):
        def qb(k, _, j=j):
            tp = ten(j)
            sp = sec(k + 1)
            tok = sp * T + tp
            rs(tok, sp * T + pt, part(tok) + got(tok), s, tp)
            return 0

        lax.fori_loop(0, S, qb, 0)

    def joined(sp):
        tok = sp * T + t
        acc = part(tok) + got(tok)
        for j in range(1, H):
            acc = acc + got(sp * T + lax.rem(pt + 2 * j, T))
        return acc

    def qc(k, _):
        sp = sec(k)
        rs(sp * T + t, s * T + pt, joined(sp), sp, t)
        return 0

    lax.fori_loop(1, S, qc, 0)
    mine = lax.fori_loop(1, S, lambda k, x: x + got(sec(-k) * T + pt), joined(s))
    out_ref[...] = (lg_ref[0] * mine).astype(jnp.bfloat16)

    sent = hbuf.at[pl.ds(0, n - 1)]
    pltpu.make_async_copy(sent, sent, ag_send).wait()
    pltpu.make_async_copy(others, others, st_ssem).wait()
    sent = sendbuf.at[pl.ds(0, n - 1)]
    pltpu.make_async_copy(sent, sent, rs_send).wait()


def solution(mesh):
    S, T = mesh.shape["section"], mesh.shape["tensor"]
    n = S * T

    def step(hidden, weight, targets, loss_grad):
        V, D = weight.shape
        C = D // LANES
        L = -(-3 * n // LANES) * LANES
        vmem, smem = pltpu.VMEM, pltpu.SMEM
        loss, grad = pl.pallas_call(
            functools.partial(kernel, S, T),
            out_shape=(
                jax.ShapeDtypeStruct((1,), jnp.float32),
                jax.ShapeDtypeStruct((C, LANES), jnp.bfloat16),
            ),
            in_specs=[
                pl.BlockSpec(memory_space=vmem),
                pl.BlockSpec(memory_space=pl.ANY),
                pl.BlockSpec(memory_space=smem),
                pl.BlockSpec(memory_space=smem),
            ],
            out_specs=(pl.BlockSpec(memory_space=smem), pl.BlockSpec(memory_space=vmem)),
            scratch_shapes=[
                vmem((V, D), jnp.bfloat16),
                vmem((n, C, LANES), jnp.bfloat16),
                vmem((n * C, LANES), jnp.float32),
                vmem((2 * n, D), jnp.float32),
                vmem((n, C, LANES), jnp.bfloat16),
                vmem((n, C, LANES), jnp.bfloat16),
                vmem((C, LANES), jnp.float32),
                vmem((1, 1, L), jnp.float32),
                vmem((n, 1, L), jnp.float32),
                pltpu.SemaphoreType.DMA((4,)),
                pltpu.SemaphoreType.DMA,
                pltpu.SemaphoreType.DMA((n,)),
                pltpu.SemaphoreType.DMA,
                pltpu.SemaphoreType.DMA,
                pltpu.SemaphoreType.DMA,
                pltpu.SemaphoreType.DMA((n,)),
            ],
            compiler_params=pltpu.CompilerParams(
                collective_id=0, has_side_effects=True, vmem_limit_bytes=67043328
            ),
        )(hidden, weight, targets, loss_grad)
        return loss, grad.reshape(1, D)

    return jax.shard_map(
        step,
        mesh=mesh,
        in_specs=(
            P(("section", "tensor"), None),
            P(("section", "tensor"), None),
            P(),
            P(("section", "tensor")),
        ),
        out_specs=(P(("section", "tensor")), P(("section", "tensor"), None)),
        check_vma=False,
    )
```

time: 245 us -> 42.4 us (0.17)
  waiting for transfers between devices: 130 us -> 0 us
  blocking collectives: 83.4 us -> 0 us
  Pallas kernels: 0 us -> 37.7 us
  matrix products: 12.1 us -> 0 us
  between operations: 14.7 us -> 3.05 us
  other arithmetic: 2.69 us -> 0 us
    unnamed x2 -> x0, waiting for transfers between devices: 130 us -> none
    all_gather x1 -> x0, blocking collectives: 46.4 us -> none  [shards(): lax.all_gather(hidden, ('section', 'tensor'), axis=0, tiled=True)]
    pallas_call x0 -> x1, Pallas kernels: none -> 37.7 us  [step(): pl.pallas_call(functools.partial(kernel, S, T), out_shape=(jax.ShapeDtype...]
    unnamed x1 -> x0, blocking collectives: 37 us -> none
    dot_general x2 -> x0, matrix products: 12.1 us -> none  [the longest x1 6.1 us: shards(): lax.dot_general(lax.all_gather(hidden, ('section', 'tensor'), axis=0, til...]
  transfers between devices with their start and end apart: 1 -> 0, of which waited for: 1 -> 0; matrix products, arithmetic and copies ran while one was open for 0% -> 0% of each run, Pallas kernels for 0% -> 0%
where the time goes in v1:
time: 42.4 us; the launch traced here: 42.1 us
  Pallas kernels  37.7 us (89%)
  between operations  3.05 us (7%)
  local copies, waits for them, and re-layouts  1.36 us (3%)
    pallas_call x1, Pallas kernels, step(): pl.pallas_call(functools.partial(kernel, S, T), out_shape=(jax.ShapeDtype...  37.7 us
    unnamed x1, local copies, waits for them, and re-layouts  1.36 us

profile of v1, /device:TPU:0, one launch (start us, length us, event | category | flops | bytes accessed | tf_op | source)
XLA Modules:
  0.0 42.1 jit_solution(16429693954757228663)
XLA Ops:
  1.3 37.7 %shard_map.59 = (f32[1]{0:T(128)}, bf16[64,128]{1,0:T(8,128)(2,1)}) custom-call(bf16[1,8192]{1,0:T(2,128)(2,1)} %hid_ref.1, bf16[512,8192]{1,0:T(8,128)(2,1)} %w_hbm.1, s32[32]{0:T(128)} %tgt_ref.1, f32[1]{0:T(128)S(6)} %copy.10.lg_ref), custom_call_target="tpu_custom_call" | custom-call | tf_op jit(solution)/shard_map/pallas_call | solution.py:253
  39.0 1.4 %copy.8 = bf16[1,1,64,128]{3,1,2,0:T(2,128)(2,1)} copy(bf16[1,1,64,128]{3,2,1,0:T(8,128)(2,1)} %bitcast.6) | data formatting | bytes 32768

commit v2 on v1

--- a/solution.py
+++ b/solution.py
@@ -12,13 +12,15 @@
 GROUP = 8
 
 
-def kernel(S, T, hid_ref, w_hbm, tgt_ref, lg_ref, loss_ref, out_ref,
+def kernel(S, T, hid_hbm, w_hbm, tgt_hbm, lg_hbm, loss_ref, out_ref,
+           hid_ref, tgt_ref, lg_ref, in_sem,
            wv, hbuf, slab, gt, sendbuf, rbuf, rowbuf, st_send, st_recv,
            w_sem, ag_send, ag_recv, st_ssem, st_rsem, rs_send, rs_recv):
     n = S * T
     H = T // 2
     V, D = wv.shape
     C = D // LANES
+    pitch = C + 8
     L = st_send.shape[2]
     s = lax.axis_index("section")
     t = lax.axis_index("tensor")
@@ -38,9 +40,6 @@
         r = pl.ds(q * rows, rows)
         return pltpu.make_async_copy(w_hbm.at[r], wv.at[r], w_sem.at[q])
 
-    for q in range(parts):
-        w_copy(q).start()
-
     barrier = pltpu.get_barrier_semaphore()
 
     def greet(k, _):
@@ -50,6 +49,15 @@
 
     lax.fori_loop(1, n, greet, 0)
 
+    hid_copy = pltpu.make_async_copy(hid_hbm, hid_ref, in_sem.at[0])
+    tgt_copy = pltpu.make_async_copy(tgt_hbm, tgt_ref, in_sem.at[1])
+    lg_copy = pltpu.make_async_copy(lg_hbm, lg_ref, in_sem.at[2])
+    hid_copy.start()
+    tgt_copy.start()
+    lg_copy.start()
+    for q in range(parts):
+        w_copy(q).start()
+    hid_copy.wait()
     own = hid_ref[...].astype(jnp.float32)
     for c in range(C):
         rowbuf[c:c + 1, :] = own[:, c * LANES:(c + 1) * LANES]
@@ -93,6 +101,8 @@
 
         lax.fori_loop(0, S, p3, 0)
 
+    tgt_copy.wait()
+    lg_copy.wait()
     tcol = lax.fori_loop(
         0, n, lambda i, x: jnp.where(lax.broadcasted_iota(jnp.int32, (n, LANES), 0) == i, tgt_ref[i], x),
         jnp.zeros((n, LANES), jnp.int32))[:, :1]
@@ -106,7 +116,7 @@
         lax.fori_loop(0, S, p4, 0)
 
     def widen(i, _):
-        slab[pl.ds(pl.multiple_of(i * C, C), C), :] = hbuf[i].astype(jnp.float32)
+        slab[pl.ds(pl.multiple_of(i * pitch, 8), C), :] = hbuf[i].astype(jnp.float32)
         return 0
 
     lax.fori_loop(0, n, widen, 0)
@@ -117,7 +127,7 @@
 
     def dot1(kc, acc):
         lhs = jnp.concatenate(
-            [slab[pl.ds(kc * GROUP + i, n, stride=C), :] for i in range(GROUP)], axis=1).astype(jnp.bfloat16)
+            [slab[pl.ds(kc * GROUP + i, n, stride=pitch), :] for i in range(GROUP)], axis=1).astype(jnp.bfloat16)
         w = wv[:, pl.ds(pl.multiple_of(kc * KC, KC), KC)]
         return acc + lax.dot_general(lhs, w, (((1,), (1,)), ((), ())), preferred_element_type=jnp.float32)
 
@@ -159,19 +169,13 @@
     others = st_recv.at[pl.ds(1, n - 1)]
     pltpu.make_async_copy(others, others, st_rsem).wait()
 
-    top = lax.fori_loop(1, n, lambda k, x: jnp.maximum(x, st_recv[k]), st_recv[0])
-
     lane = lax.broadcasted_iota(jnp.int32, (1, L), 1)
     live = lane < n
-    top = jnp.where(live, top, 0.0)
-
-    def add_live(k, carry):
-        z, g = carry
-        row = st_recv[k]
-        gap = jnp.where(live, row - top, 0.0)
-        return z + jnp.exp(gap) * pltpu.roll(row, L - n, 1), g + pltpu.roll(row, L - 2 * n, 1)
-
-    z, g = lax.fori_loop(0, n, add_live, (jnp.zeros((1, L), jnp.float32), jnp.zeros((1, L), jnp.float32)))
+    got_stats = st_recv[...]
+    top = jnp.where(live, jnp.max(got_stats, axis=0), 0.0)
+    gap = jnp.where(live[None], got_stats - top[None], 0.0)
+    z = jnp.sum(jnp.exp(gap) * pltpu.roll(got_stats, L - n, 2), axis=0)
+    g = pltpu.roll(jnp.sum(got_stats, axis=0), L - 2 * n, 1)
     z = jnp.where(live, z, 1.0)
     loss_ref[0] = jnp.sum(jnp.where(lane == me, top + jnp.log(z) - g, 0.0))
     top_c = jnp.sum(jnp.where(c == r, top, 0.0), axis=1, keepdims=True)
@@ -182,13 +186,13 @@
     def spread(kc, _):
         for i in range(GROUP):
             cols = pl.ds(pl.multiple_of(kc * KC + i * LANES, LANES), LANES)
-            slab[pl.ds(kc * GROUP + i, n, stride=C), :] = scale * gt[:n, cols] + hit * gt[n:, cols]
+            slab[pl.ds(kc * GROUP + i, n, stride=pitch), :] = scale * gt[:n, cols] + hit * gt[n:, cols]
         return 0
 
     lax.fori_loop(0, D // KC, spread, 0)
 
     def part(tok):
-        return slab[pl.ds(pl.multiple_of(tok * C, C), C), :]
+        return slab[pl.ds(pl.multiple_of(tok * pitch, 8), C), :]
 
     def rs(tok, slot, value, ds, dt):
         sendbuf[tok] = value.astype(jnp.bfloat16)
@@ -257,16 +261,17 @@
                 jax.ShapeDtypeStruct((C, LANES), jnp.bfloat16),
             ),
             in_specs=[
-                pl.BlockSpec(memory_space=vmem),
-                pl.BlockSpec(memory_space=pl.ANY),
-                pl.BlockSpec(memory_space=smem),
-                pl.BlockSpec(memory_space=smem),
-            ],
+                pl.BlockSpec(memory_space=pl.ANY)
+            ] * 4,
             out_specs=(pl.BlockSpec(memory_space=smem), pl.BlockSpec(memory_space=vmem)),
             scratch_shapes=[
+                vmem((1, D), jnp.bfloat16),
+                smem((n,), jnp.int32),
+                smem((1,), jnp.float32),
+                pltpu.SemaphoreType.DMA((3,)),
                 vmem((V, D), jnp.bfloat16),
                 vmem((n, C, LANES), jnp.bfloat16),
-                vmem((n * C, LANES), jnp.float32),
+                vmem((n * (C + 8), LANES), jnp.float32),
                 vmem((2 * n, D), jnp.float32),
                 vmem((n, C, LANES), jnp.bfloat16),
                 vmem((n, C, LANES), jnp.bfloat16),

time: 42.4 us -> 38.6 us (0.910)
  Pallas kernels: 37.7 us -> 33.9 us
    pallas_call x1, Pallas kernels: 37.7 us -> 33.9 us  [step(): pl.pallas_call(functools.partial(kernel, S, T), out_shape=(jax.ShapeDtype...]
where the time goes in v2:
time: 38.6 us; the launch traced here: 38.3 us
  Pallas kernels  33.9 us (88%)
  between operations  3.05 us (8%)
  local copies, waits for them, and re-layouts  1.36 us (4%)
    pallas_call x1, Pallas kernels, step(): pl.pallas_call(functools.partial(kernel, S, T), out_shape=(jax.ShapeDtype...  33.9 us
    unnamed x1, local copies, waits for them, and re-layouts  1.36 us

profile of v2, /device:TPU:0, one launch (start us, length us, event | category | flops | bytes accessed | tf_op | source)
XLA Modules:
  0.0 38.3 jit_solution(434498180379566323)
XLA Ops:
  1.3 33.9 %shard_map.59 = (f32[1]{0:T(128)}, bf16[64,128]{1,0:T(8,128)(2,1)}) custom-call(bf16[1,8192]{1,0:T(2,128)(2,1)} %hid_hbm.1, bf16[512,8192]{1,0:T(8,128)(2,1)} %w_hbm.1, s32[32]{0:T(128)} %tgt_hbm.1, f32[1]{0:T(128)S(6)} %copy.10.lg_hbm), custom_call_target="tpu_custom_call" | custom-call | tf_op jit(solution)/shard_map/pallas_call | solution.py:257
  35.2 1.4 %copy.8 = bf16[1,1,64,128]{3,1,2,0:T(2,128)(2,1)} copy(bf16[1,1,64,128]{3,2,1,0:T(8,128)(2,1)} %bitcast.6) | data formatting | bytes 32768

commit v3 on v2

--- a/solution.py
+++ b/solution.py
@@ -1,4 +1,5 @@
 import functools
+import math
 
 import jax
 import jax.numpy as jnp
@@ -10,6 +11,7 @@
 MESH = pl.DeviceIdType.MESH
 LANES = 128
 GROUP = 8
+WIDE = 32
 
 
 def kernel(S, T, hid_hbm, w_hbm, tgt_hbm, lg_hbm, loss_ref, out_ref,
@@ -125,13 +127,16 @@
 
     KC = GROUP * LANES
 
+    wide = math.gcd(C, WIDE)
+    span = wide * LANES
+
     def dot1(kc, acc):
         lhs = jnp.concatenate(
-            [slab[pl.ds(kc * GROUP + i, n, stride=pitch), :] for i in range(GROUP)], axis=1).astype(jnp.bfloat16)
-        w = wv[:, pl.ds(pl.multiple_of(kc * KC, KC), KC)]
+            [slab[pl.ds(kc * wide + i, n, stride=pitch), :] for i in range(wide)], axis=1).astype(jnp.bfloat16)
+        w = wv[:, pl.ds(pl.multiple_of(kc * span, span), span)]
         return acc + lax.dot_general(lhs, w, (((1,), (1,)), ((), ())), preferred_element_type=jnp.float32)
 
-    logits = lax.fori_loop(0, D // KC, dot1, jnp.zeros((n, V), jnp.float32))
+    logits = lax.fori_loop(0, D // span, dot1, jnp.zeros((n, V), jnp.float32))
 
     mask = lax.broadcasted_iota(jnp.int32, (n, V), 1) + me * V == tcol
     m = jnp.max(logits, axis=1, keepdims=True)

time: 38.6 us -> 37.9 us (0.982)
  Pallas kernels: 33.9 us -> 33.2 us
    pallas_call x1, Pallas kernels: 33.9 us -> 33.2 us  [step(): pl.pallas_call(functools.partial(kernel, S, T), out_shape=(jax.ShapeDtype...]
where the time goes in v3:
time: 37.9 us; the launch traced here: 37.6 us
  Pallas kernels  33.2 us (88%)
  between operations  3.05 us (8%)
  local copies, waits for them, and re-layouts  1.36 us (4%)
    pallas_call x1, Pallas kernels, step(): pl.pallas_call(functools.partial(kernel, S, T), out_shape=(jax.ShapeDtype...  33.2 us
    unnamed x1, local copies, waits for them, and re-layouts  1.36 us

profile of v3, /device:TPU:0, one launch (start us, length us, event | category | flops | bytes accessed | tf_op | source)
XLA Modules:
  0.0 37.6 jit_solution(6859729725414309806)
XLA Ops:
  1.3 33.2 %shard_map.59 = (f32[1]{0:T(128)}, bf16[64,128]{1,0:T(8,128)(2,1)}) custom-call(bf16[1,8192]{1,0:T(2,128)(2,1)} %hid_hbm.1, bf16[512,8192]{1,0:T(8,128)(2,1)} %w_hbm.1, s32[32]{0:T(128)} %tgt_hbm.1, f32[1]{0:T(128)S(6)} %copy.10.lg_hbm), custom_call_target="tpu_custom_call" | custom-call | tf_op jit(solution)/shard_map/pallas_call | solution.py:262
  34.5 1.4 %copy.8 = bf16[1,1,64,128]{3,1,2,0:T(2,128)(2,1)} copy(bf16[1,1,64,128]{3,2,1,0:T(8,128)(2,1)} %bitcast.6) | data formatting | bytes 32768
